TPU v7x, 32 devices: a whole 2x2x4 slice. The times are simulated.
32 devices in a mesh: dom: 16 (over z, x, core), rep: 2 (over y).
Axes of the slice: x: 2, y: 2, z: 4, core: 2. Of those that a mesh axis runs over, the one named last changes fastest.
Arguments:
- node_feats: bfloat16 [12288, 256], P(('dom', 'rep')), may hold values from -6 to 6
- node_ids: int32 [12288], replicated, may hold values from 0 to 16777215
- tile_row: int32 [16, 2, 16], replicated, may hold values from -1 to 95, as said below
- tile_col: int32 [16, 2, 16], replicated, may hold values from -1 to 95, as said below
- tile_count: int32 [16, 2, 16], replicated, may hold values from 1 to 128, as said below
- self_weight: bfloat16 [256, 512], replicated, may hold values from -0.375 to 0.375
- neigh_weight: bfloat16 [256, 512], replicated, may hold values from -3 to 3
- out_grad: bfloat16 [12288, 512], P(('dom', 'rep')), may hold values from -6 to 6
Outputs:
- hidden_out: bfloat16 [12288, 512], P(('dom', 'rep'))
- feat_grad: bfloat16 [12288, 256], P(('dom', 'rep'))
- self_grad: float32 [256, 512], replicated
- neigh_grad: float32 [256, 512], replicated
Inputs may be any that keep to these rules, and one draw needn't show every extreme that they name: `tile_row`: entry [d, r, s] is -1 where the slot holds no tile, else a block row of dom group d: d * 6 plus 0 to 5. In every draw some pair (d, r) has all 16 of its slots filled. `tile_col`: -1 exactly where tile_row is -1; else one of the blocks of device (s, r): s * 6 + r * 3 plus 0 to 2. `tile_count`: read only where a tile is present.
All inputs are finite; a program needn't handle non-finite values.
Results may differ from a plain program's by a relative error of at most 0.01.
Values may be sent and summed in bfloat16 or wider, within the bound.
A program may use at most 64 MiB of HBM per device.

v0:
```python
import math

import jax
import jax.numpy as jnp
from jax import lax
from jax.sharding import PartitionSpec as P

TILE = 128


def edge_masks(row_ids, col_ids, limits, tile_size):
    left_ids = (row_ids % 4093)[:, :, None]
    right_ids = (col_ids % 4091)[:, None, :]
    hashed = (left_ids * right_ids + left_ids + 3 * right_ids) % 4099 % tile_size
    return (hashed < limits[:, None, None]).astype(jnp.bfloat16)


def shards(
    node_feats, node_ids, tile_row, tile_col, tile_count, self_weight, neigh_weight, out_grad
):
    dom_total = lax.axis_size("dom")
    rep_total = lax.axis_size("rep")
    dom_here = lax.axis_index("dom")
    rep_here = lax.axis_index("rep")
    rows_here, width_in = node_feats.shape
    blocks_here = rows_here // TILE
    group_blocks = blocks_here * rep_total
    id_blocks = node_ids.reshape(-1, TILE)
    group_first = dom_here * group_blocks
    own_first = group_first + rep_here * blocks_here
    inbound_rows = tile_row[dom_here, rep_here]
    inbound_present = inbound_rows >= 0
    inbound_block = jnp.where(inbound_present, inbound_rows, 0)
    inbound_cols = jnp.where(inbound_present, tile_col[dom_here, rep_here], 0)
    inbound_limits = jnp.where(inbound_present, tile_count[dom_here, rep_here], 0)
    inbound_masks = edge_masks(
        id_blocks[inbound_block], id_blocks[inbound_cols], inbound_limits, TILE
    )
    inbound_offset = jnp.where(inbound_present, inbound_block - group_first, 0)
    row_select = (
        (jnp.arange(group_blocks)[:, None] == inbound_offset[None, :]) & inbound_present[None, :]
    ).astype(jnp.float32)
    outbound_cols = tile_col[:, rep_here, dom_here]
    outbound_present = outbound_cols >= 0
    outbound_offset = jnp.where(outbound_present, outbound_cols - own_first, 0)
    own_select = (
        (outbound_offset[:, None] == jnp.arange(blocks_here)[None, :]) & outbound_present[:, None]
    ).astype(jnp.float32)
    feat_blocks = node_feats.reshape(blocks_here, TILE, width_in)
    outgoing = jnp.where(
        outbound_present[:, None, None], feat_blocks[outbound_offset], jnp.zeros((), jnp.bfloat16)
    )
    products = jnp.einsum(
        "sij,sjf->sif",
        inbound_masks,
        lax.all_to_all(outgoing, "dom", split_axis=0, concat_axis=0, tiled=True),
        preferred_element_type=jnp.float32,
    )
    partial_value = jnp.einsum("bs,sif->bif", row_select, products)
    summed = lax.psum_scatter(
        partial_value.reshape(group_blocks * TILE, width_in).astype(jnp.bfloat16),
        "rep",
        scatter_dimension=0,
        tiled=True,
    ).astype(jnp.float32)
    group_rows = tile_row[dom_here].reshape(-1)
    group_limits = tile_count[dom_here].reshape(-1)
    owned_rows = group_rows[:, None] == own_first + jnp.arange(blocks_here)[None, :]
    degree = jnp.sum(jnp.where(owned_rows, group_limits[:, None], 0), axis=0).astype(jnp.float32)
    divisor = jnp.repeat(jnp.maximum(degree, 1.0), TILE)[:, None]
    mean_feats = (summed / divisor).astype(jnp.bfloat16)
    preact = jnp.dot(node_feats, self_weight, preferred_element_type=jnp.float32) + jnp.dot(
        mean_feats, neigh_weight, preferred_element_type=jnp.float32
    )
    hidden_out = jax.nn.silu(preact).astype(jnp.bfloat16)
    logistic = jax.nn.sigmoid(preact)
    pre_grad = (out_grad.astype(jnp.float32) * logistic * (1.0 + preact * (1.0 - logistic))).astype(
        jnp.bfloat16
    )
    over_rows = (((0,), (0,)), ((), ()))
    over_cols = (((1,), (1,)), ((), ()))
    self_term = lax.dot_general(node_feats, pre_grad, over_rows, preferred_element_type=jnp.float32)
    neigh_term = lax.dot_general(
        mean_feats, pre_grad, over_rows, preferred_element_type=jnp.float32
    )
    self_sum, neigh_sum = lax.psum((self_term, neigh_term), ("dom", "rep"))
    grad_scale = 1.0 / math.sqrt(rows_here * dom_total * rep_total)
    mean_grad = lax.dot_general(
        pre_grad, neigh_weight, over_cols, preferred_element_type=jnp.float32
    )
    spread = (mean_grad / divisor).astype(jnp.bfloat16)
    group_spread = lax.all_gather(spread, "rep", axis=0, tiled=True).reshape(
        group_blocks, TILE, width_in
    )
    picked_rows = group_spread[inbound_offset]
    products = jnp.einsum(
        "sij,sif->sjf", inbound_masks, picked_rows, preferred_element_type=jnp.float32
    )
    returned = lax.all_to_all(
        products.astype(jnp.bfloat16), "dom", split_axis=0, concat_axis=0, tiled=True
    ).astype(products.dtype)
    transposed = jnp.einsum("db,djf->bjf", own_select, returned)
    self_back = lax.dot_general(
        pre_grad, self_weight, over_cols, preferred_element_type=jnp.float32
    )
    feat_grad = (self_back + transposed.reshape(rows_here, width_in)).astype(jnp.bfloat16)
    return (hidden_out, feat_grad, self_sum * grad_scale, neigh_sum * grad_scale)


def solution(mesh):
    placed = (P(("dom", "rep"), None), P(), P(), P(), P(), P(), P(), P(("dom", "rep"), None))
    return jax.shard_map(
        shards,
        mesh=mesh,
        in_specs=placed,
        out_specs=(P(("dom", "rep"), None), P(("dom", "rep"), None), P(), P()),
        check_vma=False,
    )
```

profile of v0, /device:TPU:0, one launch (start us, length us, event | category | flops | bytes accessed | tf_op | source)
XLA Modules:
  0.0 234.0 jit_solution(619269368370868611)
XLA Ops:
  7.2 1.2 compare_reduce_fusion
  8.4 1.5 subtract_reduce_fusion
  9.9 1.5 gather_fusion.2
  11.4 1.1 broadcast_select_fusion
  12.5 7.5 %all-to-all-start = ((bf16[16,128,256]{2,1,0:T(8,128)(2,1)}), bf16[16,128,256]{2,1,0:T(8,128)(2,1)S(1)}, u32[]{:S(2)}, u32[]{:S(2)}) async-start(bf16[16,128,256]{2,1,0:T(8,128)(2,1)} %broadcast_select_fusion), calls=%async_computation | async-start | bytes 2097152 | tf_op jit(solution)/shard_map/all_to_all | solution.py:56
  20.1 0.7 fusion.37
  20.8 0.7 fusion.33
  22.6 0.7 constant_dynamic-slice_fusion
  23.7 0.7 fusion.36
  24.4 18.5 %all-to-all-done = bf16[16,128,256]{2,1,0:T(8,128)(2,1)S(1)} async-done(((bf16[16,128,256]{2,1,0:T(8,128)(2,1)}), bf16[16,128,256]{2,1,0:T(8,128)(2,1)S(1)}, u32[]{:S(2)}, u32[]{:S(2)}) %all-to-all-start) | async-done | bytes 1048608 | tf_op jit(solution)/shard_map/all_to_all | solution.py:56
  42.9 2.2 fusion.15
  45.9 0.8 copy.31
  47.3 14.9 %reduce-scatter.2.cloned.1.call-done = bf16[384,256]{1,0:T(8,128)(2,1)} async-done(((bf16[768,256]{1,0:T(8,128)(2,1)}), bf16[384,256]{1,0:T(8,128)(2,1)}) %reduce-scatter.2.cloned.1.call-update) | async-done | bytes 196624 | tf_op jit(solution)/shard_map/reduce_scatter | solution.py:60
  62.2 2.3 multiply_convert_fusion
  64.8 7.1 %all_gather.3 = bf16[768,256]{1,0:T(8,128)(2,1)S(1)} all-gather(bf16[384,256]{1,0:T(8,128)(2,1)S(1)} %fusion.6), channel_id=1, replica_groups=mesh['dom'=16,'rep'=2] {'rep'}, dimensions={0}, use_global_device_ids=true | all-gather | bytes 589824 | tf_op jit(solution)/shard_map/all_gather | solution.py:92
  72.6 2.9 %convolution_convert_fusion = bf16[16,128,256]{2,1,0:T(8,128)(2,1)} fusion(bf16[16,128,256]{2,1,0:T(8,128)(2,1)S(1)} %gather_fusion.3, s32[16]{0:T(128)S(1)} %get-tuple-element.31, s32[16,128]{1,0:T(8,128)S(1)} %get-tuple-element.29, s32[16,128]{1,0:T(8,128)S(1)} %get-tuple-element.28, s32[16,128]{1,0:T(8,128)S(1)} %add_select_fusion.3), kind=kOutput, calls=%fused_computation.10 | convolution fusion | flops 140247040 | bytes 2121792 | tf_op jit(solution)/shard_map/sij,sif->sjf/dot_general | solution.py:96
  75.4 5.6 %all-to-all-start.1 = ((bf16[16,128,256]{2,1,0:T(8,128)(2,1)}), bf16[16,128,256]{2,1,0:T(8,128)(2,1)S(1)}, u32[]{:S(2)}, u32[]{:S(2)}) async-start(bf16[16,128,256]{2,1,0:T(8,128)(2,1)} %convolution_convert_fusion), calls=%async_computation.2 | async-start | bytes 2097152 | tf_op jit(solution)/shard_map/all_to_all | solution.py:99
  81.1 1.1 convolution_bitcast_fusion
  82.3 1.2 fusion.45
  83.5 138.7 %all-reduce.3.cloned.1.call-done = (f32[256,512]{0,1:T(8,128)}, f32[256,512]{0,1:T(8,128)}) async-done(((f32[256,512]{0,1:T(8,128)}, f32[256,512]{0,1:T(8,128)}), (f32[256,512]{0,1:T(8,128)}, f32[256,512]{0,1:T(8,128)})) %all-reduce.3.cloned.1.call-update) | async-done | bytes 1048592 | tf_op jit(solution)/shard_map/psum | solution.py:86
  222.2 1.1 broadcast_multiply_fusion.1
  223.3 1.0 copy.35
  224.4 1.0 copy.36
  226.2 1.0 fusion.5
  (42 shorter events, 4.6 us)
Async XLA Ops:
  7.2 55.1 %copy-start = (bf16[256,512]{1,0:T(8,128)(2,1)S(1)}, bf16[256,512]{1,0:T(8,128)(2,1)}, u32[]{:S(2)}) copy-start(bf16[256,512]{1,0:T(8,128)(2,1)} %param.14) | copy-start | bytes 786436
  12.5 9.0 %copy-start.4 = (s32[12288]{0:T(1024)S(1)}, s32[12288]{0:T(1024)}, u32[]{:S(2)}) copy-start(s32[12288]{0:T(1024)} %param.9) | copy-start | bytes 147460
  12.5 30.4 %all-to-all-start = ((bf16[16,128,256]{2,1,0:T(8,128)(2,1)}), bf16[16,128,256]{2,1,0:T(8,128)(2,1)S(1)}, u32[]{:S(2)}, u32[]{:S(2)}) async-start(bf16[16,128,256]{2,1,0:T(8,128)(2,1)} %broadcast_select_fusion), calls=%async_computation | async-start | bytes 2097152 | tf_op jit(solution)/shard_map/all_to_all | solution.py:56
  20.1 42.2 %reduce-scatter.2.cloned.1.call-start = ((), (), s32[]{:S(2)}) async-start(), calls=%async_computation.3 | async-start | bytes 589824 | tf_op jit(solution)/shard_map/reduce_scatter | solution.py:60
  45.9 1.0 copy-start.1
  45.9 1.2 copy-start.2
  46.7 15.6 %copy-start.5 = (bf16[384,512]{1,0:T(8,128)(2,1)S(1)}, bf16[384,512]{1,0:T(8,128)(2,1)}, u32[]{:S(2)}) copy-start(bf16[384,512]{1,0:T(8,128)(2,1)} %param.15) | copy-start | bytes 1179652
  75.4 150.0 %all-to-all-start.1 = ((bf16[16,128,256]{2,1,0:T(8,128)(2,1)}), bf16[16,128,256]{2,1,0:T(8,128)(2,1)S(1)}, u32[]{:S(2)}, u32[]{:S(2)}) async-start(bf16[16,128,256]{2,1,0:T(8,128)(2,1)} %convolution_convert_fusion), calls=%async_computation.2 | async-start | bytes 2097152 | tf_op jit(solution)/shard_map/all_to_all | solution.py:99
  81.1 1.2 copy-start.6
  81.1 141.1 %all-reduce.3.cloned.1.call-start = ((), (), s32[]{:S(2)}) async-start(), calls=%async_computation.4 | async-start | bytes 2097152 | tf_op jit(solution)/shard_map/psum | solution.py:86
  222.2 2.1 copy-start.3
Sparse Core Ops, SparseCore 0:
  46.8 15.3 reduce-scatter.1
  87.8 134.3 all-reduce.2
where the time goes:
time: 235 us; the launch traced here: 234 us
  waiting for transfers between devices  172 us (73%)
  between operations  14.2 us (6%)
  starting transfers between devices  13.2 us (6%)
  matrix products  12.6 us (5%)
  local copies, waits for them, and re-layouts  7.39 us (3%)
  other arithmetic  7.29 us (3%)
  blocking collectives  7.14 us (3%)
    psum x1, waiting for transfers between devices, shards(): self_sum, neigh_sum = lax.psum((self_term, neigh_term), ('dom', 'rep'))  139 us
    all_to_all x1, waiting for transfers between devices, shards(): lax.all_to_all(outgoing, 'dom', split_axis=0, concat_axis=0, tiled=True)  18.5 us
    reduce_scatter x1, waiting for transfers between devices, shards(): lax.psum_scatter(partial_value.reshape(group_blocks * TILE, width_in).ast...  14.9 us
    all_to_all x1, starting transfers between devices, shards(): lax.all_to_all(outgoing, 'dom', split_axis=0, concat_axis=0, tiled=True)  7.52 us
    all_gather x1, blocking collectives, shards(): lax.all_gather(spread, 'rep', axis=0, tiled=True)  7.14 us
    all_to_all x1, starting transfers between devices, shards(): lax.all_to_all(products.astype(jnp.bfloat16), 'dom', split_axis=0, concat...  5.6 us
  transfers between devices with their start and end apart: 4, of which 3 were waited for; matrix products, arithmetic and copies ran while one was open for 4% of the time, Pallas kernels for 0%

commit v1 on v0

--- a/solution.py
+++ b/solution.py
@@ -47,9 +47,7 @@
         (outbound_offset[:, None] == jnp.arange(blocks_here)[None, :]) & outbound_present[:, None]
     ).astype(jnp.float32)
     feat_blocks = node_feats.reshape(blocks_here, TILE, width_in)
-    outgoing = jnp.where(
-        outbound_present[:, None, None], feat_blocks[outbound_offset], jnp.zeros((), jnp.bfloat16)
-    )
+    outgoing = feat_blocks[outbound_offset]
     products = jnp.einsum(
         "sij,sjf->sif",
         inbound_masks,
@@ -57,12 +55,14 @@
         preferred_element_type=jnp.float32,
     )
     partial_value = jnp.einsum("bs,sif->bif", row_select, products)
-    summed = lax.psum_scatter(
-        partial_value.reshape(group_blocks * TILE, width_in).astype(jnp.bfloat16),
+    partial_parts = lax.all_to_all(
+        partial_value.reshape(rep_total, rows_here, width_in).astype(jnp.bfloat16),
         "rep",
-        scatter_dimension=0,
+        split_axis=0,
+        concat_axis=0,
         tiled=True,
-    ).astype(jnp.float32)
+    )
+    summed = jnp.sum(partial_parts.astype(jnp.float32), axis=0)
     group_rows = tile_row[dom_here].reshape(-1)
     group_limits = tile_count[dom_here].reshape(-1)
     owned_rows = group_rows[:, None] == own_first + jnp.arange(blocks_here)[None, :]
@@ -83,8 +83,21 @@
     neigh_term = lax.dot_general(
         mean_feats, pre_grad, over_rows, preferred_element_type=jnp.float32
     )
-    self_sum, neigh_sum = lax.psum((self_term, neigh_term), ("dom", "rep"))
     grad_scale = 1.0 / math.sqrt(rows_here * dom_total * rep_total)
+    both_terms = jnp.concatenate([self_term, neigh_term], axis=0).astype(jnp.bfloat16)
+    both_rows, width_out = both_terms.shape
+    devices = dom_total * rep_total
+    both_parts = lax.all_to_all(
+        both_terms.reshape(devices, both_rows // devices, width_out),
+        ("dom", "rep"),
+        split_axis=0,
+        concat_axis=0,
+        tiled=True,
+    )
+    both_share = jnp.sum(both_parts.astype(jnp.float32), axis=0) * grad_scale
+    both_grads = lax.all_gather(
+        both_share.astype(jnp.bfloat16), ("dom", "rep"), axis=0, tiled=True
+    ).astype(jnp.float32)
     mean_grad = lax.dot_general(
         pre_grad, neigh_weight, over_cols, preferred_element_type=jnp.float32
     )
@@ -104,7 +117,7 @@
         pre_grad, self_weight, over_cols, preferred_element_type=jnp.float32
     )
     feat_grad = (self_back + transposed.reshape(rows_here, width_in)).astype(jnp.bfloat16)
-    return (hidden_out, feat_grad, self_sum * grad_scale, neigh_sum * grad_scale)
+    return (hidden_out, feat_grad, both_grads[: both_rows // 2], both_grads[both_rows // 2 :])
 
 
 def solution(mesh):

time: 235 us -> 167 us (0.71)
  waiting for transfers between devices: 172 us -> 27.3 us
  blocking collectives: 7.14 us -> 93.5 us
  between operations: 14.2 us -> 0.85 us
  starting transfers between devices: 13.2 us -> 22.6 us
  matrix products: 12.6 us -> 10.1 us
    psum x1 -> x0, waiting for transfers between devices: 139 us -> none  [shards(): self_sum, neigh_sum = lax.psum((self_term, neigh_term), ('dom', 'rep'))]
    all_gather x0 -> x1, blocking collectives: none -> 82 us  [shards(): lax.all_gather(both_share.astype(jnp.bfloat16), ('dom', 'rep'), axis=0, t...]
    reduce_scatter x1 -> x0, waiting for transfers between devices: 14.9 us -> none  [shards(): lax.psum_scatter(partial_value.reshape(group_blocks * TILE, width_in).ast...]
    all_to_all x0 -> x2, starting transfers between devices: none -> 8.94 us  [the longest x1 5.48 us: shards(): lax.all_to_all(both_terms.reshape(devices, both_rows // devices, width_ou...]
    all_to_all x0 -> x2, waiting for transfers between devices: none -> 7.63 us  [the longest x1 7.63 us: shards(): lax.all_to_all(partial_value.reshape(rep_total, rows_here, width_in).asty...]
    all_gather x1, blocking collectives: 7.14 us -> 11.5 us  [shards(): lax.all_gather(spread, 'rep', axis=0, tiled=True)]
  transfers between devices with their start and end apart: 4 -> 4, of which waited for: 3 -> 2; matrix products, arithmetic and copies ran while one was open for 4% -> 5% of each run, Pallas kernels for 0% -> 0%
where the time goes in v1:
time: 167 us
  blocking collectives  93.5 us (56%)
  waiting for transfers between devices  27.3 us (16%)
  starting transfers between devices  22.6 us (14%)
  matrix products  10.1 us (6%)
  local copies, waits for them, and re-layouts  7.21 us (4%)
  other arithmetic  5.25 us (3%)
    all_gather x1, blocking collectives, shards(): lax.all_gather(both_share.astype(jnp.bfloat16), ('dom', 'rep'), axis=0, t...  82 us
    all_to_all x1, waiting for transfers between devices, shards(): lax.all_to_all(outgoing, 'dom', split_axis=0, concat_axis=0, tiled=True)  19.6 us
    all_gather x1, blocking collectives, shards(): lax.all_gather(spread, 'rep', axis=0, tiled=True)  11.5 us
    all_to_all x1, waiting for transfers between devices, shards(): lax.all_to_all(partial_value.reshape(rep_total, rows_here, width_in).asty...  7.63 us
    all_to_all x1, starting transfers between devices, shards(): lax.all_to_all(outgoing, 'dom', split_axis=0, concat_axis=0, tiled=True)  7.52 us
    all_to_all x1, starting transfers between devices, shards(): lax.all_to_all(products.astype(jnp.bfloat16), 'dom', split_axis=0, concat...  6.18 us
    all_to_all x1, starting transfers between devices, shards(): lax.all_to_all(both_terms.reshape(devices, both_rows // devices, width_ou...  5.48 us
    all_to_all x1, starting transfers between devices, shards(): lax.all_to_all(partial_value.reshape(rep_total, rows_here, width_in).asty...  3.47 us
  transfers between devices with their start and end apart: 4, of which 2 were waited for; matrix products, arithmetic and copies ran while one was open for 5% of the time, Pallas kernels for 0%

profile of v1, /device:TPU:0, one launch (start us, length us, event | category | flops | bytes accessed | tf_op | source)
XLA Modules:
  0.0 166.8 jit_solution(14704316297488553143)
XLA Ops:
  0.7 0.7 fusion.38
  1.4 1.4 subtract_reduce_fusion
  2.8 0.7 fusion.34
  3.5 2.5 %gather_fusion.2 = bf16[16,128,256]{2,1,0:T(8,128)(2,1)} fusion(bf16[3,128,256]{2,1,0:T(8,128)(2,1)} %bitcast.71, s32[1024]{0:T(1024)S(1)} %pad_clamp_fusion.1), kind=kCustom, calls=%fused_computation.2 | custom fusion | bytes 2097216 | tf_op jit(solution)/shard_map/gather | solution.py:50
  6.0 7.5 %all-to-all-start = ((bf16[16,128,256]{2,1,0:T(8,128)(2,1)}), bf16[16,128,256]{2,1,0:T(8,128)(2,1)S(1)}, u32[]{:S(2)}, u32[]{:S(2)}) async-start(bf16[16,128,256]{2,1,0:T(8,128)(2,1)} %gather_fusion.2), calls=%async_computation | async-start | bytes 2097152 | tf_op jit(solution)/shard_map/all_to_all | solution.py:54
  14.7 0.7 constant_dynamic-slice_fusion
  15.8 0.7 fusion.37
  16.8 19.6 %all-to-all-done = bf16[16,128,256]{2,1,0:T(8,128)(2,1)S(1)} async-done(((bf16[16,128,256]{2,1,0:T(8,128)(2,1)}), bf16[16,128,256]{2,1,0:T(8,128)(2,1)S(1)}, u32[]{:S(2)}, u32[]{:S(2)}) %all-to-all-start) | async-done | bytes 1048608 | tf_op jit(solution)/shard_map/all_to_all | solution.py:54
  36.5 2.2 %fusion.16 = bf16[16,128,256]{2,1,0:T(8,128)(2,1)S(1)} fusion(bf16[16,128,256]{2,1,0:T(8,128)(2,1)S(1)} %all-to-all-done, s32[16]{0:T(128)S(1)} %get-tuple-element.15, s32[16,128]{1,0:T(8,128)S(1)} %get-tuple-element.13, s32[16,128]{1,0:T(8,128)S(1)} %get-tuple-element.12, s32[16,128]{1,0:T(8,128)S(1)} %add_select_fusion.3), kind=kOutput, calls=%fused_computation.35 | convolution fusion | flops 139722752 | bytes 2121792 | tf_op jit(solution)/shard_map/sij,sjf->sif/dot_general | solution.py:51
  38.7 0.7 fusion.2
  39.4 0.8 copy.22
  40.2 3.5 %all-to-all-start.1 = ((bf16[2,384,256]{2,1,0:T(8,128)(2,1)}), bf16[2,384,256]{2,1,0:T(8,128)(2,1)S(1)}, u32[]{:S(2)}, u32[]{:S(2)}) async-start(bf16[2,384,256]{2,1,0:T(8,128)(2,1)} %bitcast.10), calls=%async_computation.1 | async-start | bytes 786432 | tf_op jit(solution)/shard_map/all_to_all | solution.py:58
  43.7 7.6 %all-to-all-done.1 = bf16[2,384,256]{2,1,0:T(8,128)(2,1)S(1)} async-done(((bf16[2,384,256]{2,1,0:T(8,128)(2,1)}), bf16[2,384,256]{2,1,0:T(8,128)(2,1)S(1)}, u32[]{:S(2)}, u32[]{:S(2)}) %all-to-all-start.1) | async-done | bytes 393248 | tf_op jit(solution)/shard_map/all_to_all | solution.py:58
  51.5 1.3 multiply_convert_fusion
  53.6 0.8 pad_maximum_fusion
  54.4 5.5 %all-to-all-start.3 = ((bf16[32,16,512]{2,1,0:T(8,128)(2,1)}), bf16[32,16,512]{2,1,0:T(8,128)(2,1)S(1)}, u32[]{:S(2)}, u32[]{:S(2)}) async-start(bf16[32,16,512]{2,1,0:T(8,128)(2,1)} %bitcast.17), calls=%async_computation.3 | async-start | bytes 1048576 | tf_op jit(solution)/shard_map/all_to_all | solution.py:90
  60.2 11.5 %all_gather.6 = bf16[768,256]{1,0:T(8,128)(2,1)S(1)} all-gather(bf16[384,256]{1,0:T(8,128)(2,1)S(1)} %fusion.6), channel_id=1, replica_groups=mesh['dom'=16,'rep'=2] {'rep'}, dimensions={0}, use_global_device_ids=true | all-gather | bytes 589824 | tf_op jit(solution)/shard_map/all_gather | solution.py:105
  71.7 0.6 gather_fusion.3
  72.3 2.9 %convolution_convert_fusion = bf16[16,128,256]{2,1,0:T(8,128)(2,1)} fusion(bf16[16,128,256]{2,1,0:T(8,128)(2,1)S(1)} %gather_fusion.3, s32[16]{0:T(128)S(1)} %get-tuple-element.15, s32[16,128]{1,0:T(8,128)S(1)} %get-tuple-element.13, s32[16,128]{1,0:T(8,128)S(1)} %get-tuple-element.12, s32[16,128]{1,0:T(8,128)S(1)} %add_select_fusion.3), kind=kOutput, calls=%fused_computation.10 | convolution fusion | flops 140247040 | bytes 2121792 | tf_op jit(solution)/shard_map/sij,sif->sjf/dot_general | solution.py:109
  75.2 6.2 %all-to-all-start.2 = ((bf16[16,128,256]{2,1,0:T(8,128)(2,1)}), bf16[16,128,256]{2,1,0:T(8,128)(2,1)S(1)}, u32[]{:S(2)}, u32[]{:S(2)}) async-start(bf16[16,128,256]{2,1,0:T(8,128)(2,1)} %convolution_convert_fusion), calls=%async_computation.2 | async-start | bytes 2097152 | tf_op jit(solution)/shard_map/all_to_all | solution.py:112
  82.0 82.0 %all_gather.7 = bf16[512,512]{1,0:T(8,128)(2,1)S(1)} all-gather(bf16[16,512]{1,0:T(8,128)(2,1)S(1)} %multiply_convert_fusion.2), channel_id=1, replica_groups=mesh['dom'=16,'rep'=2] {'dom','rep'}, dimensions={0}, use_global_device_ids=true | all-gather | bytes 540672 | tf_op jit(solution)/shard_map/all_gather | solution.py:98
  163.9 1.1 fusion.46
  165.0 0.7 fusion.10
  165.8 1.0 fusion.5
  (39 shorter events, 3.6 us)
Async XLA Ops:
  0.6 50.8 %copy-start = (bf16[256,512]{1,0:T(8,128)(2,1)S(1)}, bf16[256,512]{1,0:T(8,128)(2,1)}, u32[]{:S(2)}) copy-start(bf16[256,512]{1,0:T(8,128)(2,1)} %param.14) | copy-start | bytes 786436
  6.0 7.5 %copy-start.3 = (s32[12288]{0:T(1024)S(1)}, s32[12288]{0:T(1024)}, u32[]{:S(2)}) copy-start(s32[12288]{0:T(1024)} %param.9) | copy-start | bytes 147460
  6.0 10.5 %copy-start.1 = (bf16[384,256]{1,0:T(8,128)(2,1)S(1)}, bf16[384,256]{1,0:T(8,128)(2,1)}, u32[]{:S(2)}) copy-start(bf16[384,256]{1,0:T(8,128)(2,1)} %param.8) | copy-start | bytes 589828
  6.0 10.5 %copy-start.2 = (bf16[256,512]{1,0:T(8,128)(2,1)S(1)}, bf16[256,512]{1,0:T(8,128)(2,1)}, u32[]{:S(2)}) copy-start(bf16[256,512]{1,0:T(8,128)(2,1)} %param.13) | copy-start | bytes 786436
  6.0 30.4 %all-to-all-start = ((bf16[16,128,256]{2,1,0:T(8,128)(2,1)}), bf16[16,128,256]{2,1,0:T(8,128)(2,1)S(1)}, u32[]{:S(2)}, u32[]{:S(2)}) async-start(bf16[16,128,256]{2,1,0:T(8,128)(2,1)} %gather_fusion.2), calls=%async_computation | async-start | bytes 2097152 | tf_op jit(solution)/shard_map/all_to_all | solution.py:54
  39.4 12.1 %copy-start.5 = (bf16[384,512]{1,0:T(8,128)(2,1)S(1)}, bf16[384,512]{1,0:T(8,128)(2,1)}, u32[]{:S(2)}) copy-start(bf16[384,512]{1,0:T(8,128)(2,1)} %param.15) | copy-start | bytes 1179652
  40.2 11.2 %all-to-all-start.1 = ((bf16[2,384,256]{2,1,0:T(8,128)(2,1)}), bf16[2,384,256]{2,1,0:T(8,128)(2,1)S(1)}, u32[]{:S(2)}, u32[]{:S(2)}) async-start(bf16[2,384,256]{2,1,0:T(8,128)(2,1)} %bitcast.10), calls=%async_computation.1 | async-start | bytes 786432 | tf_op jit(solution)/shard_map/all_to_all | solution.py:58
  54.4 20.8 %all-to-all-start.3 = ((bf16[32,16,512]{2,1,0:T(8,128)(2,1)}), bf16[32,16,512]{2,1,0:T(8,128)(2,1)S(1)}, u32[]{:S(2)}, u32[]{:S(2)}) async-start(bf16[32,16,512]{2,1,0:T(8,128)(2,1)} %bitcast.17), calls=%async_computation.3 | async-start | bytes 1048576 | tf_op jit(solution)/shard_map/all_to_all | solution.py:90
  75.2 6.2 %copy-start.4 = (s32[16,2,16]{2,1,0:T(2,128)S(1)}, s32[16,2,16]{2,1,0:T(2,128)}, u32[]{:S(2)}) copy-start(s32[16,2,16]{2,1,0:T(2,128)} %param.11) | copy-start | bytes 6148
  75.2 89.8 %all-to-all-start.2 = ((bf16[16,128,256]{2,1,0:T(8,128)(2,1)}), bf16[16,128,256]{2,1,0:T(8,128)(2,1)S(1)}, u32[]{:S(2)}, u32[]{:S(2)}) async-start(bf16[16,128,256]{2,1,0:T(8,128)(2,1)} %convolution_convert_fusion), calls=%async_computation.2 | async-start | bytes 2097152 | tf_op jit(solution)/shard_map/all_to_all | solution.py:112

commit v2 on v0

v2 whole, which is shorter than its diff:
```python
import functools
import math

import jax
import jax.numpy as jnp
from jax import lax
from jax.experimental import pallas as pl
from jax.experimental.pallas import tpu as pltpu
from jax.sharding import PartitionSpec as P

TILE = 128

MESH = pl.DeviceIdType.MESH
OVER_ROWS = (((0,), (0,)), ((), ()))
OVER_COLS = (((1,), (1,)), ((), ()))


def greet(devices):
    barrier = pltpu.get_barrier_semaphore()
    for device in devices:
        pl.semaphore_signal(barrier, inc=1, device_id=device, device_id_type=MESH)
    pl.semaphore_wait(barrier, len(devices))


def send(src, dst, sems, slot, device):
    copy = pltpu.make_async_remote_copy(
        src_ref=src,
        dst_ref=dst,
        send_sem=sems.at[0, slot],
        recv_sem=sems.at[1, slot],
        device_id=device,
        device_id_type=MESH,
    )
    copy.start()
    return copy


def dom_exchange(dom_total, src, dst, sems):
    me, rep = lax.axis_index("dom"), lax.axis_index("rep")
    peers = [lax.rem(me + k, dom_total) for k in range(1, dom_total)]
    greet([(peer, rep) for peer in peers])
    copies = [
        send(src.at[peer], dst.at[me], sems, k, (peer, rep)) for k, peer in enumerate(peers)
    ]
    dst[me] = src[me]
    for copy in copies:
        copy.wait()


def dense(
    rep_total, partials, divisor, feats, w_self, w_neigh, cotangent,
    hidden, terms, back, gathered, landed, mine, sems_in, sems_out,
):
    dom, me = lax.axis_index("dom"), lax.axis_index("rep")
    peers = [lax.rem(me + k, rep_total) for k in range(1, rep_total)]
    greet([(dom, peer) for peer in peers])
    copies = [
        send(partials.at[peer], landed.at[k], sems_in, k, (dom, peer))
        for k, peer in enumerate(peers)
    ]
    x = feats[...]
    preact = jnp.dot(x, w_self[...], preferred_element_type=jnp.float32)
    summed = partials[me].astype(jnp.float32)
    for k, copy in enumerate(copies):
        copy.wait()
        summed = summed + landed[k].astype(jnp.float32)
    div = divisor[...]
    mean = (summed / div).astype(jnp.bfloat16)
    preact = preact + jnp.dot(mean, w_neigh[...], preferred_element_type=jnp.float32)
    logistic = jax.nn.sigmoid(preact)
    grad = (
        cotangent[...].astype(jnp.float32) * logistic * (1.0 + preact * (1.0 - logistic))
    ).astype(jnp.bfloat16)
    spread = lax.dot_general(grad, w_neigh[...], OVER_COLS, preferred_element_type=jnp.float32)
    mine[...] = (spread / div).astype(jnp.bfloat16)
    copies = [
        send(mine, gathered.at[me], sems_out, k, (dom, peer)) for k, peer in enumerate(peers)
    ]
    gathered[me] = mine[...]
    hidden[...] = (preact * logistic).astype(jnp.bfloat16)
    terms[0] = lax.dot_general(
        x, grad, OVER_ROWS, preferred_element_type=jnp.float32
    ).astype(jnp.bfloat16)
    terms[1] = lax.dot_general(
        mean, grad, OVER_ROWS, preferred_element_type=jnp.float32
    ).astype(jnp.bfloat16)
    back[...] = lax.dot_general(grad, w_self[...], OVER_COLS, preferred_element_type=jnp.float32)
    for copy in copies:
        copy.wait()


def finish(
    dom_total, rep_total, inner, scale, terms, products, grads, returned,
    landed, share, strips, final, sems_a, sems_b, sems_c, sems_d, sems_e,
):
    dom, rep = lax.axis_index("dom"), lax.axis_index("rep")
    outer = dom_total // inner
    plane = inner * rep_total
    layer, within = dom // inner, lax.rem(dom, inner)
    spot = within * rep_total + rep
    plane_peers = []
    for k in range(1, plane):
        other = lax.rem(spot + k, plane)
        plane_peers.append(
            (other, (layer * inner + other // rep_total, lax.rem(other, rep_total)))
        )
    layer_peers = []
    for k in range(1, outer):
        other = lax.rem(layer + k, outer)
        layer_peers.append((other, (other * inner + within, rep)))
    dom_peers = [lax.rem(dom + k, dom_total) for k in range(1, dom_total)]
    greet([device for _, device in plane_peers] + [(peer, rep) for peer in dom_peers])
    first = [
        send(terms.at[other], landed.at[k], sems_a, k, device)
        for k, (other, device) in enumerate(plane_peers)
    ]
    exchange = [
        send(products.at[peer], returned.at[dom], sems_e, k, (peer, rep))
        for k, peer in enumerate(dom_peers)
    ]
    returned[dom] = products[dom]
    total = terms[spot].astype(jnp.float32)
    for k, copy in enumerate(first):
        copy.wait()
        total = total + landed[k].astype(jnp.float32)
    share[...] = total.astype(jnp.bfloat16)
    second = [
        send(share.at[other], strips.at[k], sems_b, k, device)
        for k, (other, device) in enumerate(layer_peers)
    ]
    total = share[layer].astype(jnp.float32)
    for k, copy in enumerate(second):
        copy.wait()
        total = total + strips[k].astype(jnp.float32)
    final[...] = (total * scale).astype(jnp.bfloat16)
    third = [
        send(final, grads.at[spot, layer], sems_c, k, device)
        for k, (_, device) in enumerate(layer_peers)
    ]
    grads[spot, layer] = final[...]
    for copy in third:
        copy.wait()
    fourth = [
        send(grads.at[spot], grads.at[spot], sems_d, k, device)
        for k, (_, device) in enumerate(plane_peers)
    ]
    for copy in fourth + exchange:
        copy.wait()


def pair_sems(count):
    return pltpu.SemaphoreType.DMA((2, max(count, 1)))


def call(kernel, out_shapes, scratch, ident, *operands):
    return pl.pallas_call(
        kernel,
        out_shape=out_shapes,
        in_specs=[pl.BlockSpec(memory_space=pltpu.VMEM)] * len(operands),
        out_specs=jax.tree.map(lambda _: pl.BlockSpec(memory_space=pltpu.VMEM), out_shapes),
        scratch_shapes=scratch,
        compiler_params=pltpu.CompilerParams(collective_id=ident, has_side_effects=True),
    )(*operands)


def edge_masks(row_ids, col_ids, limits, tile_size):
    left_ids = (row_ids % 4093)[:, :, None]
    right_ids = (col_ids % 4091)[:, None, :]
    hashed = (left_ids * right_ids + left_ids + 3 * right_ids) % 4099 % tile_size
    return (hashed < limits[:, None, None]).astype(jnp.bfloat16)


def shards(
    node_feats, node_ids, tile_row, tile_col, tile_count, self_weight, neigh_weight, out_grad
):
    dom_total = lax.axis_size("dom")
    rep_total = lax.axis_size("rep")
    dom_here = lax.axis_index("dom")
    rep_here = lax.axis_index("rep")
    rows_here, width_in = node_feats.shape
    blocks_here = rows_here // TILE
    group_blocks = blocks_here * rep_total
    id_blocks = node_ids.reshape(-1, TILE)
    group_first = dom_here * group_blocks
    own_first = group_first + rep_here * blocks_here
    inbound_rows = tile_row[dom_here, rep_here]
    inbound_present = inbound_rows >= 0
    inbound_block = jnp.where(inbound_present, inbound_rows, 0)
    inbound_cols = jnp.where(inbound_present, tile_col[dom_here, rep_here], 0)
    inbound_limits = jnp.where(inbound_present, tile_count[dom_here, rep_here], 0)
    inbound_masks = edge_masks(
        id_blocks[inbound_block], id_blocks[inbound_cols], inbound_limits, TILE
    )
    inbound_offset = jnp.where(inbound_present, inbound_block - group_first, 0)
    row_select = (
        (jnp.arange(group_blocks)[:, None] == inbound_offset[None, :]) & inbound_present[None, :]
    ).astype(jnp.float32)
    outbound_cols = tile_col[:, rep_here, dom_here]
    outbound_present = outbound_cols >= 0
    outbound_offset = jnp.where(outbound_present, outbound_cols - own_first, 0)
    own_select = (
        (outbound_offset[:, None] == jnp.arange(blocks_here)[None, :]) & outbound_present[:, None]
    ).astype(jnp.float32)
    feat_blocks = node_feats.reshape(blocks_here, TILE, width_in)
    outgoing = feat_blocks[outbound_offset]
    products = jnp.einsum(
        "sij,sjf->sif",
        inbound_masks,
        call(
            functools.partial(dom_exchange, dom_total),
            jax.ShapeDtypeStruct(outgoing.shape, jnp.bfloat16),
            [pair_sems(dom_total - 1)],
            0,
            outgoing,
        ),
        preferred_element_type=jnp.float32,
    )
    partial_value = jnp.einsum("bs,sif->bif", row_select, products)
    group_rows = tile_row[dom_here].reshape(-1)
    group_limits = tile_count[dom_here].reshape(-1)
    owned_rows = group_rows[:, None] == own_first + jnp.arange(blocks_here)[None, :]
    degree = jnp.sum(jnp.where(owned_rows, group_limits[:, None], 0), axis=0).astype(jnp.float32)
    divisor = jnp.repeat(jnp.maximum(degree, 1.0), TILE)[:, None]
    width_out = self_weight.shape[1]
    hidden_out, both_terms, self_back, group_spread = call(
        functools.partial(dense, rep_total),
        (
            jax.ShapeDtypeStruct((rows_here, width_out), jnp.bfloat16),
            jax.ShapeDtypeStruct((2, width_in, width_out), jnp.bfloat16),
            jax.ShapeDtypeStruct((rows_here, width_in), jnp.float32),
            jax.ShapeDtypeStruct((rep_total, rows_here, width_in), jnp.bfloat16),
        ),
        [
            pltpu.VMEM((max(rep_total - 1, 1), rows_here, width_in), jnp.bfloat16),
            pltpu.VMEM((rows_here, width_in), jnp.bfloat16),
            pair_sems(rep_total - 1),
            pair_sems(rep_total - 1),
        ],
        1,
        partial_value.reshape(rep_total, rows_here, width_in).astype(jnp.bfloat16),
        divisor,
        node_feats,
        self_weight,
        neigh_weight,
        out_grad,
    )
    group_spread = group_spread.reshape(group_blocks, TILE, width_in)
    grad_scale = 1.0 / math.sqrt(rows_here * dom_total * rep_total)
    picked_rows = group_spread[inbound_offset]
    products = jnp.einsum(
        "sij,sif->sjf", inbound_masks, picked_rows, preferred_element_type=jnp.float32
    )
    inner = math.gcd(dom_total, 4)
    outer = dom_total // inner
    plane = inner * rep_total
    strip = 2 * width_in // (dom_total * rep_total)
    both_grads, returned = call(
        functools.partial(finish, dom_total, rep_total, inner, grad_scale),
        (
            jax.ShapeDtypeStruct((plane, outer, strip, width_out), jnp.bfloat16),
            jax.ShapeDtypeStruct(products.shape, jnp.bfloat16),
        ),
        [
            pltpu.VMEM((max(plane - 1, 1), outer, strip, width_out), jnp.bfloat16),
            pltpu.VMEM((outer, strip, width_out), jnp.bfloat16),
            pltpu.VMEM((max(outer - 1, 1), strip, width_out), jnp.bfloat16),
            pltpu.VMEM((strip, width_out), jnp.bfloat16),
            pair_sems(plane - 1),
            pair_sems(outer - 1),
            pair_sems(outer - 1),
            pair_sems(plane - 1),
            pair_sems(dom_total - 1),
        ],
        2,
        both_terms.reshape(plane, outer, strip, width_out),
        products.astype(jnp.bfloat16),
    )
    both_grads = both_grads.reshape(2, width_in, width_out).astype(jnp.float32)
    returned = returned.astype(jnp.float32)
    transposed = jnp.einsum("db,djf->bjf", own_select, returned)
    feat_grad = (self_back + transposed.reshape(rows_here, width_in)).astype(jnp.bfloat16)
    return (hidden_out, feat_grad, both_grads[0], both_grads[1])


def solution(mesh):
    placed = (P(("dom", "rep"), None), P(), P(), P(), P(), P(), P(), P(("dom", "rep"), None))
    return jax.shard_map(
        shards,
        mesh=mesh,
        in_specs=placed,
        out_specs=(P(("dom", "rep"), None), P(("dom", "rep"), None), P(), P()),
        check_vma=False,
    )
```

time: 235 us -> 115 us (0.49)
  waiting for transfers between devices: 172 us -> 0 us
  Pallas kernels: 0 us -> 90.3 us
  between operations: 14.2 us -> 0.77 us
  starting transfers between devices: 13.2 us -> 0 us
  blocking collectives: 7.14 us -> 0 us
  matrix products: 12.6 us -> 8.21 us
  local copies, waits for them, and re-layouts: 7.39 us -> 9.83 us
    psum x1 -> x0, waiting for transfers between devices: 139 us -> none  [shards(): self_sum, neigh_sum = lax.psum((self_term, neigh_term), ('dom', 'rep'))]
    pallas_call x0 -> x3, Pallas kernels: none -> 90.3 us  [call(): pl.pallas_call(kernel, out_shape=out_shapes, in_specs=[pl.BlockSpec(memor...]
    all_to_all x2 -> x0, waiting for transfers between devices: 18.5 us -> none  [the longest x1 18.5 us: shards(): lax.all_to_all(outgoing, 'dom', split_axis=0, concat_axis=0, tiled=True)]
    reduce_scatter x1 -> x0, waiting for transfers between devices: 14.9 us -> none  [shards(): lax.psum_scatter(partial_value.reshape(group_blocks * TILE, width_in).ast...]
    all_to_all x2 -> x0, starting transfers between devices: 13.1 us -> none  [the longest x1 7.52 us: shards(): lax.all_to_all(outgoing, 'dom', split_axis=0, concat_axis=0, tiled=True)]
    all_gather x1 -> x0, blocking collectives: 7.14 us -> none  [shards(): lax.all_gather(spread, 'rep', axis=0, tiled=True)]
    dot_general x7 -> x1, matrix products: 8.38 us -> 2.73 us  [shards(): jnp.einsum('sij,sjf->sif', inbound_masks, call(functools.partial(dom_exch...]
  transfers between devices with their start and end apart: 4 -> 0, of which waited for: 3 -> 0; matrix products, arithmetic and copies ran while one was open for 4% -> 0% of each run, Pallas kernels for 0% -> 0%
where the time goes in v2:
time: 115 us
  Pallas kernels  90.3 us (79%)
  local copies, waits for them, and re-layouts  9.83 us (9%)
  matrix products  8.21 us (7%)
  other arithmetic  5.67 us (5%)
    pallas_call x3, Pallas kernels, call(): pl.pallas_call(kernel, out_shape=out_shapes, in_specs=[pl.BlockSpec(memor...  90.3 us
    dot_general x1, matrix products, shards(): jnp.einsum('sij,sif->sjf', inbound_masks, picked_rows, preferred_element_...  2.87 us
    dot_general x1, matrix products, shards(): jnp.einsum('sij,sjf->sif', inbound_masks, call(functools.partial(dom_exch...  2.73 us
    unnamed x14, local copies, waits for them, and re-layouts  2.66 us

profile of v2, /device:TPU:0, one launch (start us, length us, event | category | flops | bytes accessed | tf_op | source)
XLA Modules:
  0.0 114.8 jit_solution(10382542822655401457)
XLA Ops:
  0.7 0.8 copy-done
  1.4 1.2 %compare_reduce_fusion = pred[16]{0:T(512)(128)(4,1)S(1)} fusion(s32[16,2,16]{2,1,0:T(2,128)} %param.11, s32[]{:T(128)S(6)} %select_n.163, s32[]{:T(128)S(6)} %select_n.162), kind=kLoop, calls=%fused_computation.23 | loop fusion | flops 16 | bytes 88 | tf_op jit(solution)/shard_map/ge | solution.py:199
  2.6 1.5 %subtract_reduce_fusion = (s32[16]{0:T(128)S(1)}, s32[16]{0:T(128)S(1)}) fusion(s32[]{:T(128)S(6)} %add.127, s32[16,2,16]{2,1,0:T(2,128)} %param.11, s32[]{:T(128)S(6)} %select_n.163, s32[]{:T(128)S(6)} %select_n.162), kind=kLoop, calls=%fused_computation.28 | loop fusion | flops 48 | bytes 204 | tf_op jit(solution)/shard_map/sub | solution.py:200
  4.1 0.7 fusion.36
  4.8 0.7 fusion.35
  5.5 0.7 fusion.32
  6.1 0.7 constant_dynamic-slice_fusion
  7.3 0.6 gather_fusion
  7.9 0.6 gather_fusion.1
  8.5 0.8 copy.27
  9.3 1.6 %gather_fusion.2 = bf16[16,128,256]{2,1,0:T(8,128)(2,1)} fusion(bf16[3,128,256]{2,1,0:T(8,128)(2,1)S(1)} %bitcast.71, s32[1024]{0:T(1024)S(1)} %pad_clamp_fusion.1), kind=kCustom, calls=%fused_computation.2 | custom fusion | bytes 2097216 | tf_op jit(solution)/shard_map/gather | solution.py:205
  10.9 25.9 %shard_map.111 = bf16[16,128,256]{2,1,0:T(8,128)(2,1)} custom-call(bf16[16,128,256]{2,1,0:T(8,128)(2,1)} %gather_fusion.2), custom_call_target="tpu_custom_call" | custom-call | tf_op jit(solution)/shard_map/pallas_call | solution.py:156
  36.8 2.7 %fusion.14 = bf16[16,128,256]{2,1,0:T(8,128)(2,1)S(1)} fusion(bf16[16,128,256]{2,1,0:T(8,128)(2,1)} %shard_map.111, s32[16]{0:T(128)S(1)} %get-tuple-element.25, s32[16,128]{1,0:T(8,128)S(1)} %get-tuple-element.23, s32[16,128]{1,0:T(8,128)S(1)} %get-tuple-element.22, s32[16,128]{1,0:T(8,128)S(1)} %add_select_fusion.3), kind=kOutput, calls=%fused_computation.22 | convolution fusion | flops 139722752 | bytes 2121792 | tf_op jit(solution)/shard_map/sij,sjf->sif/dot_general | solution.py:206
  39.6 0.7 fusion.2
  40.2 0.8 copy.21
  41.1 14.9 %shard_map.112 = (bf16[384,512]{1,0:T(8,128)(2,1)}, bf16[2,256,512]{2,1,0:T(8,128)(2,1)}, f32[384,256]{1,0:T(8,128)}, bf16[2,384,256]{2,1,0:T(8,128)(2,1)}) custom-call(bf16[2,384,256]{2,1,0:T(8,128)(2,1)} %bitcast.73, f32[384,1]{1,0:T(8,128)} %bitcast.74, bf16[384,256]{1,0:T(8,128)(2,1)} %feats.1, bf16[256,512]{1,0:T(8,128)(2,1)} %w_self.1, ...), custom_call_target="tpu_custom_call" | custom-call | tf_op jit(solution)/shard_map/pallas_call | solution.py:156
  56.0 1.6 %gather_fusion.3 = bf16[16,128,256]{2,1,0:T(8,128)(2,1)S(1)} fusion(bf16[6,128,256]{2,1,0:T(8,128)(2,1)} %bitcast.72, s32[1024]{0:T(1024)S(1)} %pad_clamp_fusion), kind=kCustom, calls=%fused_computation.3 | custom fusion | bytes 2097216 | tf_op jit(solution)/shard_map/gather | solution.py:249
  57.6 2.9 %convolution_convert_fusion.products = bf16[16,128,256]{2,1,0:T(8,128)(2,1)} fusion(bf16[16,128,256]{2,1,0:T(8,128)(2,1)S(1)} %gather_fusion.3, s32[16]{0:T(128)S(1)} %get-tuple-element.25, s32[16,128]{1,0:T(8,128)S(1)} %get-tuple-element.23, s32[16,128]{1,0:T(8,128)S(1)} %get-tuple-element.22, s32[16,128]{1,0:T(8,128)S(1)} %add_select_fusion.3), kind=kOutput, calls=%fused_computation.10 | convolution fusion | flops 140247040 | bytes 2121792 | tf_op jit(solution)/shard_map/sij,sif->sjf/dot_general | solution.py:250
  60.5 49.4 %shard_map.113 = (bf16[8,4,16,512]{3,2,1,0:T(8,128)(2,1)}, bf16[16,128,256]{2,1,0:T(8,128)(2,1)}) custom-call(bf16[8,4,16,512]{3,2,1,0:T(8,128)(2,1)} %bitcast.75, bf16[16,128,256]{2,1,0:T(8,128)(2,1)} %convolution_convert_fusion.products), custom_call_target="tpu_custom_call" | custom-call | tf_op jit(solution)/shard_map/pallas_call | solution.py:156
  110.0 1.9 %fusion.7 = f32[3,128,256]{2,0,1:T(4,128)S(1)} fusion(bf16[16,128,256]{2,1,0:T(8,128)(2,1)} %get-tuple-element.14, s32[16]{0:T(128)S(1)} %get-tuple-element.29, pred[16]{0:T(512)(128)(4,1)S(1)} %compare_reduce_fusion), kind=kOutput, calls=%fused_computation.14 | convolution fusion | flops 3145824 | bytes 1441872 | tf_op jit(solution)/shard_map/db,djf->bjf/dot_general | solution.py:280
  112.0 0.7 fusion.12
  112.7 0.2 copy-done.2
  113.0 1.1 fusion.44
  114.0 0.7 copy.37
  (23 shorter events, 0.6 us)
Async XLA Ops:
  0.6 0.8 copy-start
  0.6 8.7 %copy-start.1 = (bf16[384,256]{1,0:T(8,128)(2,1)S(1)}, bf16[384,256]{1,0:T(8,128)(2,1)}, u32[]{:S(2)}) copy-start(bf16[384,256]{1,0:T(8,128)(2,1)} %feats.1) | copy-start | bytes 589828
  110.0 2.0 %copy-start.4 = (f32[384,256]{1,0:T(8,128)S(1)}, f32[384,256]{1,0:T(8,128)}, u32[]{:S(2)}) copy-start(f32[384,256]{1,0:T(8,128)} %get-tuple-element.11) | copy-start | bytes 1179652
  111.9 1.0 copy-start.2
  113.0 1.1 copy-start.3

commit v3 on v2

--- a/solution.py
+++ b/solution.py
@@ -33,18 +33,6 @@
     )
     copy.start()
     return copy
-
-
-def dom_exchange(dom_total, src, dst, sems):
-    me, rep = lax.axis_index("dom"), lax.axis_index("rep")
-    peers = [lax.rem(me + k, dom_total) for k in range(1, dom_total)]
-    greet([(peer, rep) for peer in peers])
-    copies = [
-        send(src.at[peer], dst.at[me], sems, k, (peer, rep)) for k, peer in enumerate(peers)
-    ]
-    dst[me] = src[me]
-    for copy in copies:
-        copy.wait()
 
 
 def dense(
@@ -90,8 +78,8 @@
 
 
 def finish(
-    dom_total, rep_total, inner, scale, terms, products, grads, returned,
-    landed, share, strips, final, sems_a, sems_b, sems_c, sems_d, sems_e,
+    dom_total, rep_total, inner, scale, terms, grads,
+    landed, share, strips, final, sems_a, sems_b, sems_c, sems_d,
 ):
     dom, rep = lax.axis_index("dom"), lax.axis_index("rep")
     outer = dom_total // inner
@@ -108,17 +96,11 @@
     for k in range(1, outer):
         other = lax.rem(layer + k, outer)
         layer_peers.append((other, (other * inner + within, rep)))
-    dom_peers = [lax.rem(dom + k, dom_total) for k in range(1, dom_total)]
-    greet([device for _, device in plane_peers] + [(peer, rep) for peer in dom_peers])
+    greet([device for _, device in plane_peers + layer_peers])
     first = [
         send(terms.at[other], landed.at[k], sems_a, k, device)
         for k, (other, device) in enumerate(plane_peers)
     ]
-    exchange = [
-        send(products.at[peer], returned.at[dom], sems_e, k, (peer, rep))
-        for k, peer in enumerate(dom_peers)
-    ]
-    returned[dom] = products[dom]
     total = terms[spot].astype(jnp.float32)
     for k, copy in enumerate(first):
         copy.wait()
@@ -144,7 +126,7 @@
         send(grads.at[spot], grads.at[spot], sems_d, k, device)
         for k, (_, device) in enumerate(plane_peers)
     ]
-    for copy in fourth + exchange:
+    for copy in fourth:
         copy.wait()
 
 
@@ -160,6 +142,9 @@
         out_specs=jax.tree.map(lambda _: pl.BlockSpec(memory_space=pltpu.VMEM), out_shapes),
         scratch_shapes=scratch,
         compiler_params=pltpu.CompilerParams(collective_id=ident, has_side_effects=True),
+        cost_estimate=pl.CostEstimate(
+            flops=8_000_000_000, bytes_accessed=4_000_000, transcendentals=0
+        ),
     )(*operands)
 
 
@@ -206,13 +191,7 @@
     products = jnp.einsum(
         "sij,sjf->sif",
         inbound_masks,
-        call(
-            functools.partial(dom_exchange, dom_total),
-            jax.ShapeDtypeStruct(outgoing.shape, jnp.bfloat16),
-            [pair_sems(dom_total - 1)],
-            0,
-            outgoing,
-        ),
+        lax.all_to_all(outgoing, "dom", split_axis=0, concat_axis=0, tiled=True),
         preferred_element_type=jnp.float32,
     )
     partial_value = jnp.einsum("bs,sif->bif", row_select, products)
@@ -254,12 +233,12 @@
     outer = dom_total // inner
     plane = inner * rep_total
     strip = 2 * width_in // (dom_total * rep_total)
-    both_grads, returned = call(
+    returned = lax.all_to_all(
+        products.astype(jnp.bfloat16), "dom", split_axis=0, concat_axis=0, tiled=True
+    )
+    both_grads = call(
         functools.partial(finish, dom_total, rep_total, inner, grad_scale),
-        (
-            jax.ShapeDtypeStruct((plane, outer, strip, width_out), jnp.bfloat16),
-            jax.ShapeDtypeStruct(products.shape, jnp.bfloat16),
-        ),
+        jax.ShapeDtypeStruct((plane, outer, strip, width_out), jnp.bfloat16),
         [
             pltpu.VMEM((max(plane - 1, 1), outer, strip, width_out), jnp.bfloat16),
             pltpu.VMEM((outer, strip, width_out), jnp.bfloat16),
@@ -269,11 +248,9 @@
             pair_sems(outer - 1),
             pair_sems(outer - 1),
             pair_sems(plane - 1),
-            pair_sems(dom_total - 1),
         ],
         2,
         both_terms.reshape(plane, outer, strip, width_out),
-        products.astype(jnp.bfloat16),
     )
     both_grads = both_grads.reshape(2, width_in, width_out).astype(jnp.float32)
     returned = returned.astype(jnp.float32)

time: 115 us -> 111 us (0.965)
  Pallas kernels: 90.3 us -> 53.9 us
  waiting for transfers between devices: 0 us -> 19 us
  starting transfers between devices: 0 us -> 13.7 us
  matrix products: 8.21 us -> 6.44 us
  local copies, waits for them, and re-layouts: 9.83 us -> 11 us
    pallas_call x3 -> x2, Pallas kernels: 90.3 us -> 53.9 us  [call(): pl.pallas_call(kernel, out_shape=out_shapes, in_specs=[pl.BlockSpec(memor...]
    all_to_all x0 -> x2, waiting for transfers between devices: none -> 19 us  [the longest x1 19 us: shards(): lax.all_to_all(outgoing, 'dom', split_axis=0, concat_axis=0, tiled=True)]
    all_to_all x0 -> x2, starting transfers between devices: none -> 13.7 us  [the longest x1 7.39 us: shards(): lax.all_to_all(outgoing, 'dom', split_axis=0, concat_axis=0, tiled=True)]
    dot_general x1, matrix products: 1.95 us -> 0.67 us  [shards(): transposed = jnp.einsum('db,djf->bjf', own_select, returned)]
    unnamed x14 -> x12, local copies, waits for them, and re-layouts: 2.66 us -> 1.9 us
  transfers between devices with their start and end apart: 0 -> 2, of which waited for: 0 -> 1; matrix products, arithmetic and copies ran while one was open for 0% -> 6% of each run, Pallas kernels for 0% -> 33%
where the time goes in v3:
time: 111 us; the launch traced here: 110 us
  Pallas kernels  53.9 us (49%)
  waiting for transfers between devices  19 us (17%)
  starting transfers between devices  13.7 us (12%)
  local copies, waits for them, and re-layouts  11 us (10%)
  matrix products  6.44 us (6%)
  other arithmetic  4.96 us (4%)
    pallas_call x2, Pallas kernels, call(): pl.pallas_call(kernel, out_shape=out_shapes, in_specs=[pl.BlockSpec(memor...  53.9 us
    all_to_all x1, waiting for transfers between devices, shards(): lax.all_to_all(outgoing, 'dom', split_axis=0, concat_axis=0, tiled=True)  19 us
    all_to_all x1, starting transfers between devices, shards(): lax.all_to_all(outgoing, 'dom', split_axis=0, concat_axis=0, tiled=True)  7.39 us
    all_to_all x1, starting transfers between devices, shards(): lax.all_to_all(products.astype(jnp.bfloat16), 'dom', split_axis=0, concat...  6.3 us
    dot_general x1, matrix products, shards(): jnp.einsum('sij,sif->sjf', inbound_masks, picked_rows, preferred_element_...  2.87 us
    gather x1, local copies, waits for them, and re-layouts, shards(): outgoing = feat_blocks[outbound_offset]  2.51 us
    dot_general x1, matrix products, shards(): jnp.einsum('sij,sjf->sif', inbound_masks, lax.all_to_all(outgoing, 'dom',...  2.23 us
  transfers between devices with their start and end apart: 2, of which 1 were waited for; matrix products, arithmetic and copies ran while one was open for 6% of the time, Pallas kernels for 33%

profile of v3, /device:TPU:0, one launch (start us, length us, event | category | flops | bytes accessed | tf_op | source)
XLA Modules:
  0.0 109.8 jit_solution(1526797325534571998)
XLA Ops:
  0.7 0.7 fusion.36
  1.3 1.4 %subtract_reduce_fusion = (s32[16]{0:T(128)S(1)}, s32[16]{0:T(128)S(1)}) fusion(s32[]{:T(128)S(6)} %add.127, s32[16,2,16]{2,1,0:T(2,128)} %param.11, s32[]{:T(128)S(6)} %select_n.163, s32[]{:T(128)S(6)} %select_n.162), kind=kLoop, calls=%fused_computation.28 | loop fusion | flops 48 | bytes 204 | tf_op jit(solution)/shard_map/sub | solution.py:185
  2.8 0.7 fusion.32
  3.5 2.5 %gather_fusion.2 = bf16[16,128,256]{2,1,0:T(8,128)(2,1)} fusion(bf16[3,128,256]{2,1,0:T(8,128)(2,1)} %bitcast.71, s32[1024]{0:T(1024)S(1)} %pad_clamp_fusion.1), kind=kCustom, calls=%fused_computation.2 | custom fusion | bytes 2097216 | tf_op jit(solution)/shard_map/gather | solution.py:190
  6.0 7.4 %all-to-all-start = ((bf16[16,128,256]{2,1,0:T(8,128)(2,1)}), bf16[16,128,256]{2,1,0:T(8,128)(2,1)S(1)}, u32[]{:S(2)}, u32[]{:S(2)}) async-start(bf16[16,128,256]{2,1,0:T(8,128)(2,1)} %gather_fusion.2), calls=%async_computation | async-start | bytes 2097152 | tf_op jit(solution)/shard_map/all_to_all | solution.py:194
  13.4 0.6 gather_fusion.1
  14.0 0.6 gather_fusion
  14.6 0.7 constant_dynamic-slice_fusion
  15.7 0.8 copy.31
  16.6 0.7 fusion.35
  17.3 19.0 %all-to-all-done = bf16[16,128,256]{2,1,0:T(8,128)(2,1)S(1)} async-done(((bf16[16,128,256]{2,1,0:T(8,128)(2,1)}), bf16[16,128,256]{2,1,0:T(8,128)(2,1)S(1)}, u32[]{:S(2)}, u32[]{:S(2)}) %all-to-all-start) | async-done | bytes 1048608 | tf_op jit(solution)/shard_map/all_to_all | solution.py:194
  36.3 2.2 %fusion.14 = bf16[16,128,256]{2,1,0:T(8,128)(2,1)S(1)} fusion(bf16[16,128,256]{2,1,0:T(8,128)(2,1)S(1)} %all-to-all-done, s32[16]{0:T(128)S(1)} %get-tuple-element.21, s32[16,128]{1,0:T(8,128)S(1)} %get-tuple-element.19, s32[16,128]{1,0:T(8,128)S(1)} %get-tuple-element.18, s32[16,128]{1,0:T(8,128)S(1)} %add_select_fusion.3), kind=kOutput, calls=%fused_computation.22 | convolution fusion | flops 139722752 | bytes 2121792 | tf_op jit(solution)/shard_map/sij,sjf->sif/dot_general | solution.py:191
  38.5 0.7 fusion.2
  39.2 0.8 copy.25
  40.0 17.3 %shard_map.111 = (bf16[384,512]{1,0:T(8,128)(2,1)}, bf16[2,256,512]{2,1,0:T(8,128)(2,1)}, f32[384,256]{1,0:T(8,128)}, bf16[2,384,256]{2,1,0:T(8,128)(2,1)}) custom-call(bf16[2,384,256]{2,1,0:T(8,128)(2,1)} %bitcast.75, f32[384,1]{1,0:T(8,128)} %bitcast.76, bf16[384,256]{1,0:T(8,128)(2,1)} %feats.1, bf16[256,512]{1,0:T(8,128)(2,1)} %w_self.1, ...), custom_call_target="tpu_custom_call" | custom-call | flops 8000000000 | bytes 4000000 | tf_op jit(solution)/shard_map/pallas_call | solution.py:138
  57.3 1.6 %gather_fusion.3 = bf16[16,128,256]{2,1,0:T(8,128)(2,1)S(1)} fusion(bf16[6,128,256]{2,1,0:T(8,128)(2,1)} %bitcast.72, s32[1024]{0:T(1024)S(1)} %pad_clamp_fusion), kind=kCustom, calls=%fused_computation.3 | custom fusion | bytes 2097216 | tf_op jit(solution)/shard_map/gather | solution.py:228
  58.9 2.9 %convolution_convert_fusion = bf16[16,128,256]{2,1,0:T(8,128)(2,1)} fusion(bf16[16,128,256]{2,1,0:T(8,128)(2,1)S(1)} %gather_fusion.3, s32[16]{0:T(128)S(1)} %get-tuple-element.21, s32[16,128]{1,0:T(8,128)S(1)} %get-tuple-element.19, s32[16,128]{1,0:T(8,128)S(1)} %get-tuple-element.18, s32[16,128]{1,0:T(8,128)S(1)} %add_select_fusion.3), kind=kOutput, calls=%fused_computation.10 | convolution fusion | flops 140247040 | bytes 2121792 | tf_op jit(solution)/shard_map/sij,sif->sjf/dot_general | solution.py:229
  61.8 6.3 %all-to-all-start.1 = ((bf16[16,128,256]{2,1,0:T(8,128)(2,1)}), bf16[16,128,256]{2,1,0:T(8,128)(2,1)S(1)}, u32[]{:S(2)}, u32[]{:S(2)}) async-start(bf16[16,128,256]{2,1,0:T(8,128)(2,1)} %convolution_convert_fusion), calls=%async_computation.1 | async-start | bytes 2097152 | tf_op jit(solution)/shard_map/all_to_all | solution.py:236
  68.1 0.5 compare_reduce_fusion
  68.6 36.6 %shard_map.112 = bf16[8,4,16,512]{3,2,1,0:T(8,128)(2,1)} custom-call(bf16[8,4,16,512]{3,2,1,0:T(8,128)(2,1)} %bitcast.78), custom_call_target="tpu_custom_call" | custom-call | flops 8000000000 | bytes 4000000 | tf_op jit(solution)/shard_map/pallas_call | solution.py:138
  105.2 2.1 %fusion.44 = (f32[4,4,16,512]{3,2,1,0:T(8,128)}, f32[4,4,16,512]{3,2,1,0:T(8,128)}) fusion(bf16[8,4,16,512]{3,2,1,0:T(8,128)(2,1)} %shard_map.112), kind=kLoop, calls=%fused_computation.82 | loop fusion | bytes 2097152 | tf_op jit(solution)/shard_map/slice | solution.py:259
  107.4 0.7 fusion.7
  108.3 0.7 fusion.12
  109.1 0.7 copy.41
  (25 shorter events, 0.8 us)
Async XLA Ops:
  0.6 12.8 %copy-start = (s32[12288]{0:T(1024)S(1)}, s32[12288]{0:T(1024)}, u32[]{:S(2)}) copy-start(s32[12288]{0:T(1024)} %param.9) | copy-start | bytes 147460
  6.0 30.3 %all-to-all-start = ((bf16[16,128,256]{2,1,0:T(8,128)(2,1)}), bf16[16,128,256]{2,1,0:T(8,128)(2,1)S(1)}, u32[]{:S(2)}, u32[]{:S(2)}) async-start(bf16[16,128,256]{2,1,0:T(8,128)(2,1)} %gather_fusion.2), calls=%async_computation | async-start | bytes 2097152 | tf_op jit(solution)/shard_map/all_to_all | solution.py:194
  61.8 6.3 %copy-start.3 = (s32[16,2,16]{2,1,0:T(2,128)S(1)}, s32[16,2,16]{2,1,0:T(2,128)}, u32[]{:S(2)}) copy-start(s32[16,2,16]{2,1,0:T(2,128)} %param.11) | copy-start | bytes 6148
  61.8 45.5 %all-to-all-start.1 = ((bf16[16,128,256]{2,1,0:T(8,128)(2,1)}), bf16[16,128,256]{2,1,0:T(8,128)(2,1)S(1)}, u32[]{:S(2)}, u32[]{:S(2)}) async-start(bf16[16,128,256]{2,1,0:T(8,128)(2,1)} %convolution_convert_fusion), calls=%async_computation.1 | async-start | bytes 2097152 | tf_op jit(solution)/shard_map/all_to_all | solution.py:236
  107.3 1.0 copy-start.2
  108.0 1.0 copy-start.1
